TPU v7x, 32 devices: a whole 2x2x4 slice. The times are simulated.
32 devices in a mesh: pipe: 4 (over y, core), vocab: 2 (over x), expert: 4 (over z).
Axes of the slice: x: 2, y: 2, z: 4, core: 2. Of those that a mesh axis runs over, the one named last changes fastest.
Arguments:
- token_ids: int32 [192], replicated, may hold values from 0 to 65535
- routes: int32 [192, 2], replicated, may hold values from 0 to 3, all different within a row; in each aligned block of 192 rows (0 to 191, 192 to 383, ...) at most 144 rows name the same one
- gate_weights: float32 [192, 2], replicated, may hold values from 0.2 to 1
- embed_table: bfloat16 [65536, 7168], P(('pipe', 'vocab'), 'expert'), may hold values from -0.59765625 to 0.59765625
- w_gate: bfloat16 [4, 7168, 2048], P('expert', None, ('pipe', 'vocab')), may hold values from -0.5 to 0.5
- w_up: bfloat16 [4, 7168, 2048], P('expert', None, ('pipe', 'vocab')), may hold values from -0.5 to 0.5
- w_down: bfloat16 [4, 2048, 7168], P('expert', ('pipe', 'vocab')), may hold values from -0.125 to 0.125
Outputs:
- logits: bfloat16 [192, 65536], P('expert', ('pipe', 'vocab'))
Inputs may be any that keep to these rules, and one draw needn't show every extreme that they name: `routes`: each row names 2 different experts; over all 192 rows no expert is named more than 144 times, a bound that some block reaches.
All inputs are finite; a program needn't handle non-finite values.
Results may differ from a plain program's by a relative error of at most 0.025.
Values may be sent and summed in bfloat16 or wider, within the bound.
A program may use at most 128 MiB of HBM per device.

v0:
```python
import functools

import jax
import jax.numpy as jnp
from jax import lax
from jax.experimental import pallas as pl
from jax.experimental.pallas import tpu as pltpu
from jax.sharding import PartitionSpec as P

MESH = pl.DeviceIdType.MESH
GROUP = ("pipe", "vocab")


def peer_coords(axes, sizes, index):
    coords = {}
    for axis, size in reversed(list(zip(axes, sizes))):
        coords[axis] = index % size
        index = index // size
    return coords


def exchange_kernel(axes, sizes, reduce, x_ref, o_ref, *scratch):
    n = 1
    for size in sizes:
        n *= size
    me = 0
    for axis, size in zip(axes, sizes):
        me = me * size + lax.axis_index(axis)
    if reduce:
        land, send_sem, recv_sem = scratch
    else:
        land = o_ref
        send_sem, recv_sem, local_sem = scratch
    barrier = pltpu.get_barrier_semaphore()
    for k in range(1, n):
        where = peer_coords(axes, sizes, (me + k) % n)
        pl.semaphore_signal(barrier, inc=1, device_id=where, device_id_type=MESH)
    pl.semaphore_wait(barrier, n - 1)
    copies = []
    for k in range(1, n):
        peer = (me + k) % n
        copy = pltpu.make_async_remote_copy(
            src_ref=x_ref.at[peer] if reduce else x_ref,
            dst_ref=land.at[k - 1] if reduce else land.at[me],
            send_sem=send_sem.at[k - 1],
            recv_sem=recv_sem.at[k - 1],
            device_id=peer_coords(axes, sizes, peer),
            device_id_type=MESH,
        )
        copy.start()
        copies.append(copy)
    if not reduce:
        own = pltpu.make_async_copy(x_ref, land.at[me], local_sem)
        own.start()
        own.wait()
    for copy in copies:
        copy.wait()
    if reduce:
        columns = o_ref.shape[-1]
        tile = next((t for t in (512, 256, 128) if columns % t == 0), columns)

        @pl.loop(0, columns // tile)
        def _(step):
            cols = pl.ds(pl.multiple_of(step * tile, tile), tile)
            total = x_ref[me, :, cols].astype(jnp.float32)
            for k in range(n - 1):
                total = total + land[k, :, cols].astype(jnp.float32)
            o_ref[:, cols] = total.astype(o_ref.dtype)


def exchange(x, axes, reduce, collective_id, out_dtype=None):
    sizes = tuple(lax.axis_size(axis) for axis in axes)
    n = 1
    for size in sizes:
        n *= size
    block = x.shape[1:] if reduce else x.shape
    out = jax.ShapeDtypeStruct(block if reduce else (n,) + block, out_dtype or x.dtype)
    sems = [pltpu.SemaphoreType.DMA((n - 1,)), pltpu.SemaphoreType.DMA((n - 1,))]
    if reduce:
        scratch = [pltpu.VMEM((n - 1,) + block, x.dtype)] + sems
    else:
        scratch = sems + [pltpu.SemaphoreType.DMA]
    return pl.pallas_call(
        functools.partial(exchange_kernel, axes, sizes, reduce),
        out_shape=out,
        in_specs=[pl.BlockSpec(memory_space=pltpu.VMEM)],
        out_specs=pl.BlockSpec(memory_space=pltpu.VMEM),
        scratch_shapes=scratch,
        compiler_params=pltpu.CompilerParams(collective_id=collective_id, has_side_effects=True),
    )(x)


def core_pair_kernel(sizes, reduce, x_ref, o_ref, *scratch):
    pipes, vocabs = sizes
    p, v = lax.axis_index("pipe"), lax.axis_index("vocab")
    core, me = p % 2, p * vocabs + v
    chips = pipes * vocabs // 2
    chip = (p // 2) * vocabs + v
    other = {"pipe": p + 1 - 2 * core, "vocab": v}

    def of_chip(index, on):
        pipe = (index // vocabs) * 2 + on
        return {"pipe": pipe, "vocab": index % vocabs}, pipe * vocabs + index % vocabs

    def send(src, dst, sems, at, where):
        copy = pltpu.make_async_remote_copy(
            src_ref=src, dst_ref=dst, send_sem=sems.at[0, at], recv_sem=sems.at[1, at],
            device_id=where, device_id_type=MESH,
        )
        copy.start()
        return copy

    barrier = pltpu.get_barrier_semaphore()
    pl.semaphore_signal(barrier, inc=1, device_id=other, device_id_type=MESH)
    for k in range(1, chips):
        where, _ = of_chip((chip + k) % chips, core)
        pl.semaphore_signal(barrier, inc=1, device_id=where, device_id_type=MESH)
    pl.semaphore_wait(barrier, chips)
    if not reduce:
        far, near, local_sem = scratch
        outgoing = []
        for k in range(1, chips):
            where, _ = of_chip((chip + k) % chips, core)
            outgoing.append(send(x_ref, o_ref.at[me], far, k, where))
        passed = [send(x_ref, o_ref.at[me], near, 0, other)]
        own = pltpu.make_async_copy(x_ref, o_ref.at[me], local_sem)
        own.start()
        for k in range(1, chips):
            outgoing[k - 1].wait_recv()
            _, source = of_chip((chip + chips - k) % chips, core)
            passed.append(send(o_ref.at[source], o_ref.at[source], near, k, other))
        own.wait()
        for copy in outgoing:
            copy.wait_send()
        for copy in passed:
            copy.wait()
        return
    paired, merged, land, far, near = scratch
    columns = o_ref.shape[-1]
    tile = next((t for t in (512, 256, 128) if columns % t == 0), columns)

    def each_tile(body):
        @pl.loop(0, columns // tile)
        def _(step):
            body(pl.ds(pl.multiple_of(step * tile, tile), tile))

    given = []
    order = list(range(1, chips)) + [0]
    for k in order:
        _, index = of_chip((chip + k) % chips, 1 - core)
        given.append(send(x_ref.at[index], paired.at[k], near, k, other))
    outgoing, ready = [], None
    for copy, k in zip(given, order):
        copy.wait_recv()
        where, index = of_chip((chip + k) % chips, core)

        def merge(cols):
            total = x_ref[index, :, cols].astype(jnp.float32)
            total = total + paired[k, :, cols].astype(jnp.float32)
            merged[k, :, cols] = total.astype(merged.dtype)

        if k:
            each_tile(merge)
        if ready is not None:
            at, to = ready
            outgoing.append(send(merged.at[at], land.at[at], far, at, to))
        ready = (k, where)
    for copy in given:
        copy.wait_send()
    for copy in outgoing:
        copy.wait()

    def finish(cols):
        total = x_ref[me, :, cols].astype(jnp.float32) + paired[0, :, cols].astype(jnp.float32)
        for k in range(1, chips):
            total = total + land[k, :, cols].astype(jnp.float32)
        o_ref[:, cols] = total.astype(o_ref.dtype)

    each_tile(finish)


def core_pair_exchange(x, reduce, collective_id):
    sizes = tuple(lax.axis_size(axis) for axis in GROUP)
    n = sizes[0] * sizes[1]
    chips = n // 2
    block = x.shape[1:] if reduce else x.shape
    pair_sems = [pltpu.SemaphoreType.DMA((2, chips)), pltpu.SemaphoreType.DMA((2, chips))]
    if reduce:
        scratch = [pltpu.VMEM((chips,) + block, x.dtype)] * 3 + pair_sems
    else:
        scratch = pair_sems + [pltpu.SemaphoreType.DMA]
    return pl.pallas_call(
        functools.partial(core_pair_kernel, sizes, reduce),
        out_shape=jax.ShapeDtypeStruct(block if reduce else (n,) + block, x.dtype),
        in_specs=[pl.BlockSpec(memory_space=pltpu.VMEM)],
        out_specs=pl.BlockSpec(memory_space=pltpu.VMEM),
        scratch_shapes=scratch,
        compiler_params=pltpu.CompilerParams(collective_id=collective_id, has_side_effects=True),
    )(x)


def logits_kernel(n, steps, x_ref, table_ref, o_ref, held, land, send_sem, recv_sem):
    step = pl.program_id(0)
    me = lax.axis_index("expert")
    part, tile = held.shape[1], table_ref.shape[0]

    def sends(at):
        cols = pl.ds(pl.multiple_of(at * tile, tile), tile)
        return [
            pltpu.make_async_remote_copy(
                src_ref=held.at[(me + k) % n, :, cols],
                dst_ref=land.at[k - 1, :, cols],
                send_sem=send_sem.at[k - 1, at],
                recv_sem=recv_sem.at[k - 1, at],
                device_id={"expert": (me + k) % n},
                device_id_type=MESH,
            )
            for k in range(1, n)
        ]

    @pl.when(step == 0)
    def _():
        barrier = pltpu.get_barrier_semaphore()
        for k in range(1, n):
            pl.semaphore_signal(
                barrier, inc=1, device_id={"expert": (me + k) % n}, device_id_type=MESH
            )
        pl.semaphore_wait(barrier, n - 1)

    @pl.when(step > 0)
    def _():
        for copy in sends(step - 1):
            copy.start()

    block = lax.dot_general(
        x_ref[...], table_ref[...], (((1,), (1,)), ((), ())), preferred_element_type=jnp.float32
    ).astype(held.dtype)
    here = pl.ds(pl.multiple_of(step * tile, tile), tile)
    for i in range(n):
        held[i, :, here] = block[i * part : (i + 1) * part]

    @pl.when(step == steps - 1)
    def _():
        for copy in sends(steps - 1):
            copy.start()

        @pl.loop(0, steps)
        def _(at):
            for copy in sends(at):
                copy.wait()
            cols = pl.ds(pl.multiple_of(at * tile, tile), tile)
            total = held[me, :, cols].astype(jnp.float32)
            for k in range(n - 1):
                total = total + land[k, :, cols].astype(jnp.float32)
            o_ref[:, cols] = total.astype(o_ref.dtype)


def logits_sum(residual, table, collective_id):
    n = lax.axis_size("expert")
    (tokens, width), rows = residual.shape, table.shape[0]
    part, tile = tokens // n, 512
    steps = rows // tile
    return pl.pallas_call(
        functools.partial(logits_kernel, n, steps),
        grid=(steps,),
        out_shape=jax.ShapeDtypeStruct((part, rows), residual.dtype),
        in_specs=[
            pl.BlockSpec((tokens, width), lambda i: (0, 0)),
            pl.BlockSpec((tile, width), lambda i: (i, 0)),
        ],
        out_specs=pl.BlockSpec((part, rows), lambda i: (0, 0)),
        scratch_shapes=[
            pltpu.VMEM((n, part, rows), residual.dtype),
            pltpu.VMEM((n - 1, part, rows), residual.dtype),
            pltpu.SemaphoreType.DMA((n - 1, steps)),
            pltpu.SemaphoreType.DMA((n - 1, steps)),
        ],
        compiler_params=pltpu.CompilerParams(
            collective_id=collective_id, has_side_effects=True,
            dimension_semantics=("arbitrary",),
        ),
    )(residual, table)


def per_device(token_ids, routes, gate_weights, embed_table, w_gate, w_up, w_down):
    vocab_rows, width_cols = embed_table.shape
    tokens = routes.shape[0]
    experts = lax.axis_size("expert")
    group = lax.axis_size(GROUP)
    width = experts * width_cols
    part = tokens // group
    row_base = lax.axis_index(GROUP) * vocab_rows
    local_ids = token_ids - row_base
    in_shard = (local_ids >= 0) & (local_ids < vocab_rows)
    rows = embed_table.at[jnp.clip(local_ids, 0, vocab_rows - 1)].get(mode="promise_in_bounds")
    rows = jnp.where(in_shard[:, None], rows, jnp.zeros_like(rows))
    own = exchange(rows.reshape(group, part, width_cols), GROUP, True, 0)
    wide = exchange(own, ("expert",), False, 1)
    wide = wide.transpose(1, 0, 2).reshape(part, width)
    embedded = core_pair_exchange(wide, False, 2).reshape(tokens, width)
    gate_proj = jnp.dot(embedded, w_gate[0], preferred_element_type=jnp.float32)
    up_proj = jnp.dot(embedded, w_up[0], preferred_element_type=jnp.float32)
    hidden = (jax.nn.silu(gate_proj) * up_proj).astype(jnp.bfloat16)
    share = jnp.sum(
        jnp.where(routes == lax.axis_index("expert"), gate_weights, 0.0), axis=1, keepdims=True
    )
    partial_out = jnp.dot(hidden, w_down[0], preferred_element_type=jnp.float32) * share
    partial_out = partial_out.astype(jnp.bfloat16).reshape(group, part, width)
    summed = core_pair_exchange(partial_out, True, 3)
    summed = summed.reshape(part, experts, width_cols).transpose(1, 0, 2)
    moe_out = exchange(summed, ("expert",), True, 4, jnp.float32)
    residual = (own.astype(jnp.float32) + moe_out).astype(jnp.bfloat16)
    residual = exchange(residual, GROUP, False, 5).reshape(tokens, width_cols)
    return logits_sum(residual, embed_table, 6)


def solution(mesh):
    return jax.shard_map(
        per_device,
        mesh=mesh,
        in_specs=(
            P(),
            P(),
            P(),
            P(GROUP, "expert"),
            P("expert", None, GROUP),
            P("expert", None, GROUP),
            P("expert", GROUP, None),
        ),
        out_specs=P("expert", GROUP),
        check_vma=False,
    )
```

profile of v0, /device:TPU:0, one launch (start us, length us, event | category | flops | bytes accessed | tf_op | source)
XLA Modules:
  0.0 211.6 jit_solution(10999699516463456529)
XLA Ops:
  0.0 0.7 fusion.20
  0.7 0.7 compare_and_fusion
  1.4 0.7 compare_select_fusion.1
  2.1 0.1 broadcast_in_dim.22
  2.2 14.9 %gather_fusion = bf16[192,1792]{1,0:T(8,128)(2,1)S(1)} fusion(bf16[8192,1792]{1,0:T(8,128)(2,1)} %table_ref.1, s32[1024]{0:T(1024)S(1)} %pad_clamp_fusion), kind=kCustom, calls=%fused_computation | custom fusion | bytes 1377024 | tf_op jit(solution)/shard_map/gather | solution.py:295
  17.1 1.0 broadcast_select_fusion.x_ref
  18.0 14.8 %shard_map.73.x_ref = bf16[24,1792]{1,0:T(8,128)(2,1)} custom-call(bf16[8,24,1792]{2,1,0:T(8,128)(2,1)} %broadcast_select_fusion.x_ref), custom_call_target="tpu_custom_call" | custom-call | tf_op jit(solution)/shard_map/pallas_call | solution.py:83
  32.9 12.0 %shard_map.74 = bf16[4,24,1792]{2,1,0:T(8,128)(2,1)} custom-call(bf16[24,1792]{1,0:T(8,128)(2,1)} %shard_map.73.x_ref), custom_call_target="tpu_custom_call" | custom-call | tf_op jit(solution)/shard_map/pallas_call | solution.py:83
  44.9 1.7 copy.12
  46.6 22.4 %shard_map.75 = bf16[8,24,7168]{2,1,0:T(8,128)(2,1)} custom-call(bf16[24,7168]{1,0:T(8,128)(2,1)} %bitcast.36), custom_call_target="tpu_custom_call" | custom-call | tf_op jit(solution)/shard_map/pallas_call | solution.py:192
  69.0 0.0 copy-start
  69.0 3.9 %fusion.4 = f32[192,256]{1,0:T(8,128)S(1)} fusion(bf16[192,7168]{1,0:T(8,128)(2,1)} %bitcast.31, bf16[1,7168,256]{2,1,0:T(8,128)(2,1)} %param.11), kind=kOutput, calls=%fused_computation.6 | convolution fusion | flops 704643072 | bytes 6619136 | tf_op jit(solution)/shard_map/dot_general | solution.py:301
  72.9 0.0 copy-done
  72.9 7.8 %fusion = bf16[192,7168]{1,0:T(8,128)(2,1)} fusion(bf16[1,256,7168]{2,1,0:T(8,128)(2,1)} %param.13, f32[192]{0:T(256)S(1)} %fusion.20, bf16[192,7168]{1,0:T(8,128)(2,1)S(1)} %bitcast.32, bf16[1,7168,256]{2,1,0:T(8,128)(2,1)} %param.12, f32[192,256]{1,0:T(8,128)S(1)} %fusion.4), kind=kOutput, calls=%fused_computation.2 | convolution fusion | flops 1412333568 | bytes 13042432 | tf_op jit(solution)/shard_map/dot_general | solution.py:307
  80.7 0.0 copy-start.1
  80.7 23.8 %shard_map.76 = bf16[24,7168]{1,0:T(8,128)(2,1)} custom-call(bf16[8,24,7168]{2,1,0:T(8,128)(2,1)} %bitcast.33), custom_call_target="tpu_custom_call" | custom-call | tf_op jit(solution)/shard_map/pallas_call | solution.py:192
  104.6 1.7 copy.14
  106.3 12.8 %shard_map.77 = f32[24,1792]{1,0:T(8,128)} custom-call(bf16[4,24,1792]{2,1,0:T(8,128)(2,1)} %bitcast.38), custom_call_target="tpu_custom_call" | custom-call | tf_op jit(solution)/shard_map/pallas_call | solution.py:83
  119.1 0.0 copy-done.1
  119.1 1.6 add_convert_fusion.x_ref
  120.7 13.1 %shard_map.78 = bf16[8,24,1792]{2,1,0:T(8,128)(2,1)} custom-call(bf16[24,1792]{1,0:T(8,128)(2,1)} %add_convert_fusion.x_ref), custom_call_target="tpu_custom_call" | custom-call | tf_op jit(solution)/shard_map/pallas_call | solution.py:83
  133.8 75.7 %shard_map.79 = bf16[48,8192]{1,0:T(8,128)(2,1)} custom-call(bf16[192,1792]{1,0:T(8,128)(2,1)} %bitcast.35, bf16[8192,1792]{1,0:T(8,128)(2,1)} %table_ref.1), custom_call_target="tpu_custom_call" | custom-call | tf_op jit(solution)/shard_map/pallas_call | solution.py:263
  209.5 2.1 copy.16
  (1 shorter events, 0.0 us)
Async XLA Ops:
  69.0 3.9 %copy-start = (bf16[8,24,7168]{2,1,0:T(8,128)(2,1)S(1)}, bf16[8,24,7168]{2,1,0:T(8,128)(2,1)}, u32[]{:S(2)}) copy-start(bf16[8,24,7168]{2,1,0:T(8,128)(2,1)} %shard_map.75) | copy-start | bytes 8257540
  80.7 38.4 %copy-start.1 = (bf16[24,1792]{1,0:T(8,128)(2,1)S(1)}, bf16[24,1792]{1,0:T(8,128)(2,1)}, u32[]{:S(2)}) copy-start(bf16[24,1792]{1,0:T(8,128)(2,1)} %shard_map.73.x_ref) | copy-start | bytes 258052
where the time goes:
time: 212 us
  Pallas kernels  175 us (83%)
  local copies, waits for them, and re-layouts  20.5 us (10%)
  matrix products  11.7 us (6%)
  other arithmetic  4.63 us (2%)
    pallas_call x1, Pallas kernels, logits_sum(): pl.pallas_call(functools.partial(logits_kernel, n, steps), grid=(steps,),...  75.7 us
    pallas_call x4, Pallas kernels, exchange(): pl.pallas_call(functools.partial(exchange_kernel, axes, sizes, reduce), o...  52.7 us
    pallas_call x2, Pallas kernels, core_pair_exchange(): pl.pallas_call(functools.partial(core_pair_kernel, sizes, reduce), out_sh...  46.2 us
    gather x1, local copies, waits for them, and re-layouts, per_device(): embed_table.at[jnp.clip(local_ids, 0, vocab_rows - 1)]  14.9 us
    dot_general x1, matrix products, per_device(): jnp.dot(hidden, w_down[0], preferred_element_type=jnp.float32) * share  7.79 us

commit v1 on v0

v1 whole, which is shorter than its diff:
```python
import functools

import jax
import jax.numpy as jnp
from jax import lax
from jax.experimental import pallas as pl
from jax.experimental.pallas import tpu as pltpu
from jax.sharding import PartitionSpec as P

MESH = pl.DeviceIdType.MESH
GROUP = ("pipe", "vocab")
VMEM_LIMIT = 67043328
LAG, HOP_LAG = 4, 2


def fused_kernel(
    dims, x_ref, share_ref, gate_ref, up_ref, down_ref, table_ref, o_ref,
    gate, up, down, tiles, scatter, mine, emb, paired, landed, summed, spread, res, held, right, left,
    w_sem, t_sem, a_sem, b_sem, c_sem, n_sem, p_sem, d_sem, e_sem, f_sem, g_sem, r_sem, l_sem,
):
    pipes, vocabs, experts, groups, rows, width, tile, steps, buffers = dims
    chips = pipes * vocabs // 2
    size = 2 * chips
    p, v, e = lax.axis_index("pipe"), lax.axis_index("vocab"), lax.axis_index("expert")
    core, chip = p % 2, (p // 2) * vocabs + v
    me = core * chips + chip
    tokens = size * rows
    dest_rows = tokens // experts
    f32 = jnp.float32

    def at_rank(rank):
        on, where = rank // chips, rank % chips
        return {"pipe": (where // vocabs) * 2 + on, "vocab": where % vocabs}

    def remote(src, dst, sems, index, where):
        return pltpu.make_async_remote_copy(
            src_ref=src, dst_ref=dst, send_sem=sems.at[(0,) + index], recv_sem=sems.at[(1,) + index],
            device_id=where, device_id_type=MESH,
        )

    def weight_copies():
        copies = [
            pltpu.make_async_copy(gate_ref, gate, w_sem.at[0]),
            pltpu.make_async_copy(up_ref, up, w_sem.at[1]),
        ]
        for b in range(experts):
            if len(down_ref.shape) == 2:
                src = down_ref.at[:, b * width : (b + 1) * width]
            else:
                src = down_ref.at[b]
            copies.append(pltpu.make_async_copy(src, down.at[b], w_sem.at[2 + b]))
        return copies

    def tile_copy(s):
        t = s % steps
        return pltpu.make_async_copy(
            table_ref.at[pl.ds(pl.multiple_of(t * tile, tile), tile), :],
            tiles.at[s % buffers],
            t_sem.at[s % buffers],
        )

    barrier = pltpu.get_barrier_semaphore()
    for k in range(1, size):
        pl.semaphore_signal(barrier, inc=1, device_id=at_rank((me + k) % size), device_id_type=MESH)
    for k in range(1, experts):
        pl.semaphore_signal(barrier, inc=1, device_id={"expert": (e + k) % experts}, device_id_type=MESH)
    weights = weight_copies()
    for copy in weights:
        copy.start()
    for s in range(buffers - 1):
        tile_copy(s).start()
    pl.semaphore_wait(barrier, size + experts - 2)

    def scatter_copies(k):
        return [
            remote(x_ref.at[k, (me + i) % size], scatter.at[k, i - 1], a_sem, (k, i - 1), at_rank((me + i) % size))
            for i in range(1, size)
        ]

    def spread_copies(k):
        return [
            remote(
                mine.at[k], emb.at[k, e, me], b_sem, (k, i - 1), {"expert": (e + i) % experts}
            )
            for i in range(1, experts)
        ]

    def plane_copies(k, i):
        b = (e + experts - i) % experts
        src = mine.at[k] if i == 0 else emb.at[k, b, me]
        out = [
            remote(src, emb.at[k, b, me], c_sem, (k, i, c - 1), at_rank(core * chips + (chip + c) % chips))
            for c in range(1, chips)
        ]
        near = remote(src, emb.at[k, b, me], n_sem, (k, i, 0), at_rank((1 - core) * chips + chip))
        return out, near

    def passed_copy(k, i, c):
        b = (e + experts - i) % experts
        at = core * chips + (chip + chips - c) % chips
        return remote(emb.at[k, b, at], emb.at[k, b, at], n_sem, (k, i, c), at_rank((1 - core) * chips + chip))

    def pair_copy(k, b):
        return remote(
            emb.at[k, b, pl.ds((1 - core) * chips, chips)], paired.at[k, b], p_sem, (k, b),
            at_rank((1 - core) * chips + chip),
        )

    def reduce_copies(k, b):
        out = []
        for c in range(1, chips):
            to = core * chips + (chip + c) % chips
            out.append(remote(emb.at[k, b, to], landed.at[k, c - 1, b], d_sem, (k, b, c - 1), at_rank(to)))
        return out

    def expert_copies(k):
        return [
            remote(
                summed.at[k, (e + i) % experts], spread.at[k, i - 1], e_sem, (k, i - 1),
                {"expert": (e + i) % experts},
            )
            for i in range(1, experts)
        ]

    def residual_copies(k):
        out = [
            remote(res.at[k, me], res.at[k, me], f_sem, (k, c - 1), at_rank(core * chips + (chip + c) % chips))
            for c in range(1, chips)
        ]
        near = remote(res.at[k, me], res.at[k, me], g_sem, (k, 0), at_rank((1 - core) * chips + chip))
        return out, near

    def residual_passed(k, c):
        at = core * chips + (chip + chips - c) % chips
        return remote(res.at[k, at], res.at[k, at], g_sem, (k, c), at_rank((1 - core) * chips + chip))

    def start_scatter(k):
        for copy in scatter_copies(k):
            copy.start()

    def own_rows(k):
        total = x_ref[k, me].astype(f32)
        for copy in scatter_copies(k):
            copy.wait_recv()
        for i in range(size - 1):
            total = total + scatter[k, i].astype(f32)
        value = total.astype(mine.dtype)
        mine[k] = value
        emb[k, e, me] = value
        for copy in spread_copies(k):
            copy.start()
        out, near = plane_copies(k, 0)
        for copy in out:
            copy.start()
        near.start()

    def gather_rows(k):
        spreads = spread_copies(k)
        for i in range(1, experts):
            spreads[i - 1].wait_recv()
            out, near = plane_copies(k, i)
            for copy in out:
                copy.start()
            near.start()

    def pass_rows(k):
        for i in range(experts):
            out, _ = plane_copies(k, i)
            for c in range(1, chips):
                out[c - 1].wait_recv()
                passed_copy(k, i, c).start()

    def expert_layer(k):
        gate_sum = jnp.zeros((tokens, gate.shape[1]), f32)
        up_sum = gate_sum
        for i in range(experts):
            _, near = plane_copies(k, i)
            near.wait_recv()
            for c in range(1, chips):
                passed_copy(k, i, c).wait_recv()
            b = (e + experts - i) % experts
            block = emb[k, b].reshape(tokens, width)
            here = pl.ds(pl.multiple_of(b * width, width), width)
            gate_sum = gate_sum + jnp.dot(block, gate[here, :], preferred_element_type=f32)
            up_sum = up_sum + jnp.dot(block, up[here, :], preferred_element_type=f32)
        hidden = (jax.nn.silu(gate_sum) * up_sum).astype(emb.dtype)
        for copy in spread_copies(k):
            copy.wait_send()
        for i in range(experts):
            out, near = plane_copies(k, i)
            for copy in out:
                copy.wait_send()
            near.wait_send()
            for c in range(1, chips):
                passed_copy(k, i, c).wait_send()
        share = share_ref[k]
        for b in range(experts):
            value = jnp.dot(hidden, down[b], preferred_element_type=f32) * share
            emb[k, b] = value.astype(emb.dtype).reshape(size, rows, width)
            if b > 0:
                pair_copy(k, b - 1).start()
        pair_copy(k, experts - 1).start()

    def merge_pairs(k):
        for b in range(experts):
            pair_copy(k, b).wait_recv()
            for c in range(chips):
                at = core * chips + c
                emb[k, b, at] = (emb[k, b, at].astype(f32) + paired[k, b, c].astype(f32)).astype(emb.dtype)
            for copy in reduce_copies(k, b):
                copy.start()

    def sum_rows(k):
        for i in range(1, experts + 1):
            b = (e + i) % experts
            for copy in reduce_copies(k, b):
                copy.wait_recv()
            total = emb[k, b, me].astype(f32)
            for c in range(chips - 1):
                total = total + landed[k, c, b].astype(f32)
            summed[k, b] = total.astype(summed.dtype)
            if i < experts:
                expert_copies(k)[i - 1].start()

    def residual(k):
        total = summed[k, e].astype(f32)
        for i, copy in enumerate(expert_copies(k)):
            copy.wait_recv()
            total = total + spread[k, i].astype(f32)
        res[k, me] = (total + mine[k].astype(f32)).astype(res.dtype)
        out, near = residual_copies(k)
        for copy in out:
            copy.start()
        near.start()

    def gather_residual(k):
        out, near = residual_copies(k)
        for c in range(1, chips):
            out[c - 1].wait_recv()
            residual_passed(k, c).start()
        near.wait_recv()
        for c in range(1, chips):
            residual_passed(k, c).wait_recv()

    def columns(t):
        return pl.ds(pl.multiple_of(t * tile, tile), tile)

    def right_copy(k, d, t, first):
        src = (held if first else right).at[k, d, :, columns(t)]
        return remote(
            src, right.at[k, d, :, columns(t)], r_sem, (k, d, t), {"expert": (e + 1) % experts}
        )

    def left_copy(k, d, t, first):
        src = (held if first else left).at[k, d, :, columns(t)]
        return remote(
            src, left.at[k, d, :, columns(t)], l_sem, (k, d, t), {"expert": (e + experts - 1) % experts}
        )

    total_steps = groups * steps

    def forward(s):
        at_right = s - LAG - HOP_LAG * (e - 1)

        @pl.when((e > 0) & (at_right >= 0) & (at_right < total_steps))
        def _():
            k, t = at_right // steps, at_right % steps

            @pl.loop(0, experts - 1 - e)
            def _(i):
                d = experts - 1 - i
                right_copy(k, d, t, False).wait_recv()
                cols = columns(t)
                value = right[k, d, :, cols].astype(f32) + held[k, d, :, cols].astype(f32)
                right[k, d, :, cols] = value.astype(right.dtype)
                right_copy(k, d, t, False).start()

        at_left = s - LAG - HOP_LAG * (experts - 2 - e)

        @pl.when((e < experts - 1) & (at_left >= 0) & (at_left < total_steps))
        def _():
            k, t = at_left // steps, at_left % steps

            @pl.loop(0, e)
            def _(d):
                left_copy(k, d, t, False).wait_recv()
                cols = columns(t)
                value = left[k, d, :, cols].astype(f32) + held[k, d, :, cols].astype(f32)
                left[k, d, :, cols] = value.astype(left.dtype)
                left_copy(k, d, t, False).start()

        at_end = s - LAG - HOP_LAG * (experts - 2)

        @pl.when((at_end >= 0) & (at_end < total_steps))
        def _():
            k, t = at_end // steps, at_end % steps
            cols = columns(t)
            out_rows = pl.ds(pl.multiple_of(k * dest_rows, dest_rows), dest_rows)
            own = held[k, e, :, cols].astype(f32)

            @pl.when(e == 0)
            def _():
                left_copy(k, e, t, False).wait_recv()
                o_ref[out_rows, cols] = (own + left[k, e, :, cols].astype(f32)).astype(o_ref.dtype)

            @pl.when(e == experts - 1)
            def _():
                right_copy(k, e, t, False).wait_recv()
                o_ref[out_rows, cols] = (own + right[k, e, :, cols].astype(f32)).astype(o_ref.dtype)

            @pl.when((e > 0) & (e < experts - 1))
            def _():
                right_copy(k, e, t, False).wait_recv()
                left_copy(k, e, t, False).wait_recv()
                total = own + right[k, e, :, cols].astype(f32) + left[k, e, :, cols].astype(f32)
                o_ref[out_rows, cols] = total.astype(o_ref.dtype)

    def logits(k):
        @pl.loop(0, steps)
        def _(t):
            s = k * steps + t

            @pl.when(s + buffers - 1 < total_steps)
            def _():
                tile_copy(s + buffers - 1).start()

            tile_copy(s).wait()
            block = lax.dot_general(
                res[k].reshape(tokens, width), tiles[s % buffers], (((1,), (1,)), ((), ())),
                preferred_element_type=f32,
            ).astype(held.dtype)
            cols = columns(t)
            for d in range(experts):
                held[k, d, :, cols] = block[d * dest_rows : (d + 1) * dest_rows]

            @pl.when(e == 0)
            def _():
                @pl.loop(0, experts - 1)
                def _(i):
                    right_copy(k, experts - 1 - i, t, True).start()

            @pl.when(e == experts - 1)
            def _():
                @pl.loop(0, experts - 1)
                def _(i):
                    left_copy(k, i, t, True).start()

            forward(s)

    for k in range(groups):
        start_scatter(k)
    for k in range(groups):
        own_rows(k)
    for copy in weights:
        copy.wait()
    for k in range(groups):
        gather_rows(k)
    for k in range(groups):
        pass_rows(k)
        expert_layer(k)
        merge_pairs(k)
    for k in range(min(2, groups)):
        sum_rows(k)
    for k in range(groups):
        residual(k)
        gather_residual(k)
        if k > 0 and k + 1 < groups:
            sum_rows(k + 1)
        logits(k)

    @pl.loop(total_steps, total_steps + LAG + HOP_LAG * (experts - 2))
    def _(s):
        forward(s)

    for k in range(groups):
        for copy in scatter_copies(k):
            copy.wait_send()
        for b in range(experts):
            pair_copy(k, b).wait_send()
            for copy in reduce_copies(k, b):
                copy.wait_send()
        for copy in expert_copies(k):
            copy.wait_send()
        out, near = residual_copies(k)
        for copy in out:
            copy.wait_send()
        near.wait_send()
        for c in range(1, chips):
            residual_passed(k, c).wait_send()

    @pl.loop(0, total_steps)
    def _(s):
        k, t = s // steps, s % steps

        @pl.loop(0, experts - 1 - e)
        def _(i):
            right_copy(k, experts - 1 - i, t, True).wait_send()

        @pl.loop(0, e)
        def _(d):
            left_copy(k, d, t, True).wait_send()


def fused(x, share, gate, up, down, table, collective_id):
    pipes, vocabs, experts = (lax.axis_size(axis) for axis in ("pipe", "vocab", "expert"))
    groups, size, rows, width = x.shape
    chips = size // 2
    vocab_rows = table.shape[0]
    part = groups * size * rows // experts
    dest_rows = part // groups
    tile = next(t for t in (1024, 512, 256, 128) if vocab_rows % t == 0)
    steps, buffers = vocab_rows // tile, 3
    hidden = gate.shape[1]
    dims = (pipes, vocabs, experts, groups, rows, width, tile, steps, buffers)
    dma = pltpu.SemaphoreType.DMA
    bf16 = x.dtype
    anywhere = pl.BlockSpec(memory_space=pl.ANY)
    inside = pl.BlockSpec(memory_space=pltpu.VMEM)
    return pl.pallas_call(
        functools.partial(fused_kernel, dims),
        out_shape=jax.ShapeDtypeStruct((part, vocab_rows), bf16),
        in_specs=[inside, inside, anywhere, anywhere, anywhere, anywhere],
        out_specs=inside,
        scratch_shapes=[
            pltpu.VMEM(gate.shape, bf16),
            pltpu.VMEM(up.shape, bf16),
            pltpu.VMEM((experts, hidden, width), bf16),
            pltpu.VMEM((buffers, tile, width), bf16),
            pltpu.VMEM((groups, size - 1, rows, width), bf16),
            pltpu.VMEM((groups, rows, width), bf16),
            pltpu.VMEM((groups, experts, size, rows, width), bf16),
            pltpu.VMEM((groups, experts, chips, rows, width), bf16),
            pltpu.VMEM((groups, chips - 1, experts, rows, width), bf16),
            pltpu.VMEM((groups, experts, rows, width), bf16),
            pltpu.VMEM((groups, experts - 1, rows, width), bf16),
            pltpu.VMEM((groups, size, rows, width), bf16),
            pltpu.VMEM((groups, experts, dest_rows, vocab_rows), bf16),
            pltpu.VMEM((groups, experts, dest_rows, vocab_rows), bf16),
            pltpu.VMEM((groups, experts, dest_rows, vocab_rows), bf16),
            dma((2 + experts,)),
            dma((buffers,)),
            dma((2, groups, size - 1)),
            dma((2, groups, experts - 1)),
            dma((2, groups, experts, chips - 1)),
            dma((2, groups, experts, chips)),
            dma((2, groups, experts)),
            dma((2, groups, experts, chips - 1)),
            dma((2, groups, experts - 1)),
            dma((2, groups, chips - 1)),
            dma((2, groups, chips)),
            dma((2, groups, experts, steps)),
            dma((2, groups, experts, steps)),
        ],
        compiler_params=pltpu.CompilerParams(
            collective_id=collective_id, has_side_effects=True, vmem_limit_bytes=VMEM_LIMIT
        ),
    )(x, share, gate, up, down, table)


def token_groups(tokens, size, experts):
    for groups in (3, 2, 1):
        if tokens % (groups * size * 8) == 0 and tokens % (groups * experts * 8) == 0:
            return groups
    return 1


def per_device(token_ids, routes, gate_weights, embed_table, w_gate, w_up, w_down):
    vocab_rows, width = embed_table.shape
    tokens = routes.shape[0]
    experts = lax.axis_size("expert")
    size = lax.axis_size(GROUP)
    groups = token_groups(tokens, size, experts)
    rows = tokens // groups // size

    def regroup(x):
        split = x.reshape((experts, groups, tokens // groups // experts) + x.shape[1:])
        return jnp.swapaxes(split, 0, 1).reshape(x.shape)

    row_base = lax.axis_index(GROUP) * vocab_rows
    local_ids = regroup(token_ids) - row_base
    in_shard = (local_ids >= 0) & (local_ids < vocab_rows)
    x = embed_table.at[jnp.clip(local_ids, 0, vocab_rows - 1)].get(mode="promise_in_bounds")
    x = jnp.where(in_shard[:, None], x, jnp.zeros_like(x)).reshape(groups, size, rows, width)
    share = jnp.sum(
        jnp.where(routes == lax.axis_index("expert"), gate_weights, 0.0), axis=1, keepdims=True
    )
    share = regroup(share).reshape(groups, size * rows, 1)
    down = w_down[0]
    if width % 128:
        down = down.reshape(down.shape[0], experts, width).transpose(1, 0, 2)
    return fused(x, share, w_gate[0], w_up[0], down, embed_table, 0)


def solution(mesh):
    return jax.shard_map(
        per_device,
        mesh=mesh,
        in_specs=(
            P(),
            P(),
            P(),
            P(GROUP, "expert"),
            P("expert", None, GROUP),
            P("expert", None, GROUP),
            P("expert", GROUP, None),
        ),
        out_specs=P("expert", GROUP),
        check_vma=False,
    )
```

time: 212 us -> 138 us (0.65)
  Pallas kernels: 175 us -> 117 us
  matrix products: 11.7 us -> 0 us
  local copies, waits for them, and re-layouts: 20.5 us -> 18.1 us
    pallas_call x7 -> x1, Pallas kernels: 175 us -> 117 us  [fused(): pl.pallas_call(functools.partial(fused_kernel, dims), out_shape=jax.Shape...]
    dot_general x2 -> x0, matrix products: 11.7 us -> none  [the longest x1 7.79 us: per_device(): jnp.dot(hidden, w_down[0], preferred_element_type=jnp.float32) * share]
    reshape x2 -> x0, local copies, waits for them, and re-layouts: 3.46 us -> none  [the longest x1 1.73 us: per_device(): wide = wide.transpose(1, 0, 2).reshape(part, width)]
where the time goes in v1:
time: 138 us
  Pallas kernels  117 us (85%)
  local copies, waits for them, and re-layouts  18.1 us (13%)
  other arithmetic  3.07 us (2%)
    pallas_call x1, Pallas kernels, fused(): pl.pallas_call(functools.partial(fused_kernel, dims), out_shape=jax.Shape...  117 us
    gather x1, local copies, waits for them, and re-layouts, per_device(): embed_table.at[jnp.clip(local_ids, 0, vocab_rows - 1)]  14.9 us

profile of v1, /device:TPU:0, one launch (start us, length us, event | category | flops | bytes accessed | tf_op | source)
XLA Modules:
  0.0 138.0 jit_solution(7725843828930953099)
XLA Ops:
  0.0 0.7 fusion
  0.7 0.7 compare_and_fusion
  1.4 0.7 subtract_clamp_fusion
  2.1 0.1 reshape.60
  2.2 0.1 and.18
  2.3 0.1 min.16
  2.4 0.1 min.18
  2.5 0.1 reshape_broadcast_in_dim.3
  2.6 0.7 reshape_reshape.4.share_ref
  3.3 14.9 %gather_fusion = bf16[192,1792]{1,0:T(8,128)(2,1)S(1)} fusion(bf16[8192,1792]{1,0:T(8,128)(2,1)} %table_ref.1, s32[1024]{0:T(1024)S(1)} %pad_clamp_fusion), kind=kCustom, calls=%fused_computation | custom fusion | bytes 1377024 | tf_op jit(solution)/shard_map/gather | solution.py:482
  18.2 1.0 broadcast_select_fusion.x_ref
  19.2 116.7 %shard_map.73 = bf16[48,8192]{1,0:T(8,128)(2,1)} custom-call(bf16[3,8,8,1792]{3,2,1,0:T(8,128)(2,1)} %broadcast_select_fusion.x_ref, f32[3,64,1]{2,1,0:T(8,128)} %reshape_reshape.4.share_ref, bf16[7168,256]{1,0:T(8,128)(2,1)} %bitcast.10, bf16[7168,256]{1,0:T(8,128)(2,1)} %bitcast.11, bf16[256,7168]{1,0:T(8,128)(2,1)} %bitcast.12, bf16[8192,1792]{1,0:T(8,128)(2,1)} %table_ref.1), custom_call_target="tpu_custom_call" | custom-call | tf_op jit(solution)/shard_map/pallas_call | solution.py:419
  135.9 2.1 %copy.16 = bf16[48,8192]{1,0:T(8,128)(2,1)} copy(bf16[48,8192]{1,0:T(8,128)(2,1)} %shard_map.73) | data formatting | bytes 1572864
  (5 shorter events, 0.0 us)

commit v2 on v1

v2 whole, which is shorter than its diff:
```python
import functools
import math

import jax
import jax.numpy as jnp
from jax import lax
from jax.experimental import pallas as pl
from jax.experimental.pallas import tpu as pltpu
from jax.sharding import PartitionSpec as P

MESH = pl.DeviceIdType.MESH
GROUP = ("pipe", "vocab")
VMEM_LIMIT, VMEM_ROOM, VMEM_SPARE = 67043328, 13 * 2**20, 8 * 2**20
LAG, HOP_LAG = 6, 2


def fused_kernel(
    dims, x_ref, share_ref, gate_ref, up_ref, down_ref, table_ref, o_ref,
    gate, up, down, tiles, scatter, mine, emb, paired, landed, summed, spread, res, held, right, left,
    w_sem, t_sem, a_sem, b_sem, c_sem, n_sem, p_sem, d_sem, e_sem, f_sem, g_sem, x_sem, sent_rows, sent,
):
    pipes, vocabs, experts, groups, rows, width, tile, steps, buffers = dims
    chips = pipes * vocabs // 2
    size = 2 * chips
    p, v, e = lax.axis_index("pipe"), lax.axis_index("vocab"), lax.axis_index("expert")
    core, chip = p % 2, (p // 2) * vocabs + v
    me = core * chips + chip
    tokens = size * rows
    dest_rows = tokens // experts
    f32 = jnp.float32

    def at_rank(rank):
        on, where = rank // chips, rank % chips
        return {"pipe": (where // vocabs) * 2 + on, "vocab": where % vocabs}

    def remote(src, dst, send_sem, recv_sem, where):
        return pltpu.make_async_remote_copy(
            src_ref=src, dst_ref=dst, send_sem=send_sem, recv_sem=recv_sem,
            device_id=where, device_id_type=MESH,
        )

    def settle(ref, sem):
        pltpu.make_async_copy(ref, ref, sem).wait()

    def weight_copies():
        copies = [
            pltpu.make_async_copy(gate_ref, gate, w_sem.at[0]),
            pltpu.make_async_copy(up_ref, up, w_sem.at[1]),
        ]
        for b in range(experts):
            if len(down_ref.shape) == 2:
                src = down_ref.at[:, b * width : (b + 1) * width]
            else:
                src = down_ref.at[b]
            copies.append(pltpu.make_async_copy(src, down.at[b], w_sem.at[2]))
        return copies

    def tile_copy(s):
        t = s % steps
        return pltpu.make_async_copy(
            table_ref.at[pl.ds(pl.multiple_of(t * tile, tile), tile), :],
            tiles.at[s % buffers],
            t_sem.at[s % buffers],
        )

    barrier = pltpu.get_barrier_semaphore()
    for k in range(1, size):
        pl.semaphore_signal(barrier, inc=1, device_id=at_rank((me + k) % size), device_id_type=MESH)
    for k in range(1, experts):
        pl.semaphore_signal(barrier, inc=1, device_id={"expert": (e + k) % experts}, device_id_type=MESH)
    weights = weight_copies()
    for copy in weights:
        copy.start()
    for s in range(buffers - 1):
        tile_copy(s).start()
    pl.semaphore_wait(barrier, size + experts - 2)

    partner = at_rank((1 - core) * chips + chip)

    def same_core(c):
        return core * chips + (chip + c) % chips

    def start_scatter(k):
        for i in range(1, size):
            to = (me + i) % size
            remote(x_ref.at[k, to], scatter.at[k, i - 1], sent.at[0], a_sem.at[k], at_rank(to)).start()

    def send_plane(k, i):
        b = (e + experts - i) % experts
        src = mine.at[k] if i == 0 else emb.at[k, b, me]
        for c in range(1, chips):
            remote(src, emb.at[k, b, me], sent_rows.at[k], c_sem.at[k, i], at_rank(same_core(c))).start()
        remote(src, emb.at[k, b, me], sent_rows.at[k], n_sem.at[k, i], partner).start()

    def own_rows(k):
        total = x_ref[k, me].astype(f32)
        settle(scatter.at[k], a_sem.at[k])
        for i in range(size - 1):
            total = total + scatter[k, i].astype(f32)
        value = total.astype(mine.dtype)
        mine[k] = value
        emb[k, e, me] = value
        for i in range(1, experts):
            remote(
                mine.at[k], emb.at[k, e, me], sent.at[1], b_sem.at[k, i - 1], {"expert": (e + i) % experts}
            ).start()
        send_plane(k, 0)

    def gather_rows(k):
        for i in range(1, experts):
            b = (e + experts - i) % experts
            settle(emb.at[k, b, me], b_sem.at[k, i - 1])
            send_plane(k, i)

    def pass_rows(k):
        for i in range(experts):
            b = (e + experts - i) % experts
            settle(emb.at[k, b, pl.ds(0, chips - 1)], c_sem.at[k, i])
            for c in range(1, chips):
                block = emb.at[k, b, same_core(c)]
                remote(block, block, sent_rows.at[k], n_sem.at[k, i], partner).start()

    def expert_layer(k):
        gate_sum = jnp.zeros((tokens, gate.shape[1]), f32)
        up_sum = gate_sum
        for i in range(experts):
            b = (e + experts - i) % experts
            settle(emb.at[k, b, pl.ds(0, chips)], n_sem.at[k, i])
            block = emb[k, b].reshape(tokens, width)
            here = pl.ds(pl.multiple_of(b * width, width), width)
            gate_sum = gate_sum + jnp.dot(block, gate[here, :], preferred_element_type=f32)
            up_sum = up_sum + jnp.dot(block, up[here, :], preferred_element_type=f32)
        hidden = (jax.nn.silu(gate_sum) * up_sum).astype(emb.dtype)
        settle(emb.at[k, :, pl.ds(0, size - 1)], sent_rows.at[k])
        share = share_ref[k]

        def send_pair(b):
            away = emb.at[k, b, pl.ds((1 - core) * chips, chips)]
            remote(away, paired.at[k, b], sent.at[2], p_sem.at[k, b], partner).start()

        for b in range(experts):
            value = jnp.dot(hidden, down[b], preferred_element_type=f32) * share
            emb[k, b] = value.astype(emb.dtype).reshape(size, rows, width)
            if b > 0:
                send_pair(b - 1)
        send_pair(experts - 1)

    def merge_pairs(k):
        for b in range(experts):
            settle(paired.at[k, b], p_sem.at[k, b])
            for c in range(chips):
                at = core * chips + c
                emb[k, b, at] = (emb[k, b, at].astype(f32) + paired[k, b, c].astype(f32)).astype(emb.dtype)
            for c in range(1, chips):
                to = same_core(c)
                remote(emb.at[k, b, to], landed.at[k, b, c - 1], sent.at[3], d_sem.at[k, b], at_rank(to)).start()

    def sum_rows(k):
        for i in range(1, experts + 1):
            b = (e + i) % experts
            settle(landed.at[k, b], d_sem.at[k, b])
            total = emb[k, b, me].astype(f32)
            for c in range(chips - 1):
                total = total + landed[k, b, c].astype(f32)
            summed[k, b] = total.astype(summed.dtype)
            if i < experts:
                remote(summed.at[k, b], spread.at[k, i - 1], sent.at[4], e_sem.at[k], {"expert": b}).start()

    def residual(k):
        total = summed[k, e].astype(f32)
        settle(spread.at[k], e_sem.at[k])
        for i in range(experts - 1):
            total = total + spread[k, i].astype(f32)
        res[k, me] = (total + mine[k].astype(f32)).astype(res.dtype)
        block = res.at[k, me]
        for c in range(1, chips):
            remote(block, block, sent.at[5], f_sem.at[k], at_rank(same_core(c))).start()
        remote(block, block, sent.at[5], g_sem.at[k], partner).start()

    def gather_residual(k):
        settle(res.at[k, pl.ds(0, chips - 1)], f_sem.at[k])
        for c in range(1, chips):
            block = res.at[k, same_core(c)]
            remote(block, block, sent.at[5], g_sem.at[k], partner).start()

    def whole_residual(k):
        settle(res.at[k, pl.ds(0, chips)], g_sem.at[k])

    def columns(t):
        return pl.ds(pl.multiple_of(t * tile, tile), tile)

    def right_copy(k, d, t, first):
        src = (held if first else right).at[k, d, :, columns(t)]
        return remote(
            src, right.at[k, d, :, columns(t)], sent.at[6], x_sem.at[k, d + 1, t], {"expert": (e + 1) % experts}
        )

    def left_copy(k, d, t, first):
        src = (held if first else left).at[k, d, :, columns(t)]
        return remote(
            src, left.at[k, d, :, columns(t)], sent.at[6], x_sem.at[k, d, t], {"expert": (e + experts - 1) % experts}
        )

    total_steps = groups * steps
    last = groups - 1
    early_steps = last * steps
    last_rounds = max(1, experts - 2)

    def add_right(k, d, t):
        right_copy(k, d, t, False).wait_recv()
        cols = columns(t)
        value = right[k, d, :, cols].astype(f32) + held[k, d, :, cols].astype(f32)
        right[k, d, :, cols] = value.astype(right.dtype)
        right_copy(k, d, t, False).start()

    def add_left(k, d, t):
        left_copy(k, d, t, False).wait_recv()
        cols = columns(t)
        value = left[k, d, :, cols].astype(f32) + held[k, d, :, cols].astype(f32)
        left[k, d, :, cols] = value.astype(left.dtype)
        left_copy(k, d, t, False).start()

    def forward(s):
        at_right = s - LAG - HOP_LAG * (e - 1)

        @pl.when((e > 0) & (at_right >= 0) & (at_right < total_steps))
        def _():
            @pl.loop(0, experts - 1 - e)
            def _(i):
                add_right(at_right // steps, experts - 1 - i, at_right % steps)

        at_left = s - LAG - HOP_LAG * (experts - 2 - e)

        @pl.when((e < experts - 1) & (at_left >= 0) & (at_left < total_steps))
        def _():
            @pl.loop(0, e)
            def _(d):
                add_left(at_left // steps, d, at_left % steps)

        at_end = s - LAG - HOP_LAG * (experts - 2)

        @pl.when((at_end >= 0) & (at_end < early_steps))
        def _():
            finish(at_end // steps, at_end % steps)

    def finish(k, t):
        cols = columns(t)
        out_rows = pl.ds(pl.multiple_of(k * dest_rows, dest_rows), dest_rows)
        own = held[k, e, :, cols].astype(f32)

        @pl.when(e == 0)
        def _():
            left_copy(k, e, t, False).wait_recv()
            o_ref[out_rows, cols] = (own + left[k, e, :, cols].astype(f32)).astype(o_ref.dtype)

        @pl.when(e == experts - 1)
        def _():
            right_copy(k, e, t, False).wait_recv()
            o_ref[out_rows, cols] = (own + right[k, e, :, cols].astype(f32)).astype(o_ref.dtype)

        @pl.when((e > 0) & (e < experts - 1))
        def _():
            right_copy(k, e, t, False).wait_recv()
            left_copy(k, e, t, False).wait_recv()
            total = own + right[k, e, :, cols].astype(f32) + left[k, e, :, cols].astype(f32)
            o_ref[out_rows, cols] = total.astype(o_ref.dtype)

    def logits(k):
        @pl.loop(0, steps)
        def _(t):
            s = k * steps + t

            @pl.when(s + buffers - 1 < total_steps)
            def _():
                tile_copy(s + buffers - 1).start()

            tile_copy(s).wait()
            block = lax.dot_general(
                res[k].reshape(tokens, width), tiles[s % buffers], (((1,), (1,)), ((), ())),
                preferred_element_type=f32,
            ).astype(held.dtype)
            cols = columns(t)
            for d in range(experts):
                held[k, d, :, cols] = block[d * dest_rows : (d + 1) * dest_rows]

            rounds = last_rounds if k == last else experts - 1

            @pl.when(e == 0)
            def _():
                @pl.loop(0, rounds)
                def _(i):
                    right_copy(k, experts - 1 - i, t, True).start()

            @pl.when(e == experts - 1)
            def _():
                @pl.loop(0, rounds)
                def _(i):
                    left_copy(k, i, t, True).start()

            forward(s)

    def run(phase, k):
        with jax.named_scope(phase.__name__ + str(k)):
            phase(k)

    first = min(2, groups)
    for k in range(first):
        run(start_scatter, k)
    run(own_rows, 0)
    for k in range(first, groups):
        run(start_scatter, k)
    for k in range(1, first):
        run(own_rows, k)
    run(gather_rows, 0)
    for k in range(first, groups):
        run(own_rows, k)
    for k in range(1, first):
        run(gather_rows, k)
    settle(gate, w_sem.at[0])
    settle(up, w_sem.at[1])
    settle(down, w_sem.at[2])
    run(pass_rows, 0)
    run(expert_layer, 0)
    run(merge_pairs, 0)
    for k in range(first, groups):
        run(gather_rows, k)
    for k in range(1, first):
        run(pass_rows, k)
        run(expert_layer, k)
        run(merge_pairs, k)
    run(sum_rows, 0)
    for k in range(first, groups):
        run(pass_rows, k)
    run(residual, 0)
    for k in range(first, groups):
        run(expert_layer, k)
    run(gather_residual, 0)
    for k in range(first, groups):
        run(merge_pairs, k)
    for k in range(1, first):
        run(sum_rows, k)
    for k in range(groups):
        if k > 0:
            run(residual, k)
            run(gather_residual, k)
        run(whole_residual, k)
        if k > 0 and k + 1 < groups:
            run(sum_rows, k + 1)
        run(logits, k)

    @pl.when(e == 0)
    def _():
        @pl.loop(last_rounds * steps, (experts - 1) * steps)
        def _(j):
            right_copy(last, experts - 1 - j // steps, j % steps, True).start()

    @pl.when(e == experts - 1)
    def _():
        @pl.loop(last_rounds * steps, (experts - 1) * steps)
        def _(j):
            left_copy(last, j // steps, j % steps, True).start()

    @pl.loop(total_steps, total_steps + LAG + HOP_LAG * (experts - 2))
    def _(s):
        with jax.named_scope("epi"):
            forward(s)

    with jax.named_scope("last"):
        @pl.loop(0, steps)
        def _(t):
            finish(last, t)

    settle(scatter, sent.at[0])
    settle(spread, sent.at[1])
    settle(paired, sent.at[2])
    settle(landed, sent.at[3])
    settle(spread, sent.at[4])
    settle(res.at[:, pl.ds(0, size - 1)], sent.at[5])
    settle(held.at[:, pl.ds(0, experts - 1)], sent.at[6])


def fused(x, share, gate, up, down, table, collective_id):
    pipes, vocabs, experts = (lax.axis_size(axis) for axis in ("pipe", "vocab", "expert"))
    groups, size, rows, width = x.shape
    chips = size // 2
    vocab_rows = table.shape[0]
    part = groups * size * rows // experts
    dest_rows = part // groups
    tile = next(t for t in (1024, 512, 256, 128) if vocab_rows % t == 0)
    steps, buffers = vocab_rows // tile, 3
    hidden = gate.shape[1]
    dims = (pipes, vocabs, experts, groups, rows, width, tile, steps, buffers)
    dma = pltpu.SemaphoreType.DMA
    bf16 = x.dtype
    away = pl.BlockSpec(memory_space=pl.ANY)
    inside = pl.BlockSpec(memory_space=pltpu.VMEM)
    buffered = [
        gate.shape,
        up.shape,
        (experts, hidden, width),
        (buffers, tile, width),
        (groups, size - 1, rows, width),
        (groups, rows, width),
        (groups, experts, size, rows, width),
        (groups, experts, chips, rows, width),
        (groups, experts, chips - 1, rows, width),
        (groups, experts, rows, width),
        (groups, experts - 1, rows, width),
        (groups, size, rows, width),
        (groups, experts, dest_rows, vocab_rows),
        (groups, experts, dest_rows, vocab_rows),
        (groups, experts, dest_rows, vocab_rows),
    ]
    held = sum(2 * math.prod(shape[:-1]) * -(-shape[-1] // 128) * 128 for shape in buffered)
    return pl.pallas_call(
        functools.partial(fused_kernel, dims),
        out_shape=jax.ShapeDtypeStruct((part, vocab_rows), bf16),
        in_specs=[inside, inside, away, away, away, away],
        out_specs=inside,
        scratch_shapes=[pltpu.VMEM(shape, bf16) for shape in buffered] + [
            dma((3,)),
            dma((buffers,)),
            dma((groups,)),
            dma((groups, experts - 1)),
            dma((groups, experts)),
            dma((groups, experts)),
            dma((groups, experts)),
            dma((groups, experts)),
            dma((groups,)),
            dma((groups,)),
            dma((groups,)),
            dma((groups, experts + 1, steps)),
            dma((groups,)),
            dma((7,)),
        ],
        compiler_params=pltpu.CompilerParams(
            collective_id=collective_id, has_side_effects=True,
            vmem_limit_bytes=min(VMEM_LIMIT, max(VMEM_LIMIT - VMEM_ROOM, held + VMEM_SPARE)),
        ),
    )(x, share, gate, up, down, table)


def gather_kernel(dims, ids_ref, lane_ids_ref, routes_ref, weights_ref, table_ref, x_ref, share_ref, fetched, sem):
    groups, size, rows, experts, block = dims
    tokens = ids_ref.shape[0]
    width = table_ref.shape[1]
    each = tokens // groups
    dest_rows = each // experts
    shard_rows = table_ref.shape[0]
    base = (lax.axis_index("pipe") * lax.axis_size("vocab") + lax.axis_index("vocab")) * shard_rows

    @pl.loop(0, tokens, unroll=8)
    def _(t):
        row = ids_ref[t] - base
        row = jnp.where((row >= 0) & (row < shard_rows), row, t * block)
        first = pl.multiple_of((row // block) * block, block)
        pltpu.make_async_copy(
            table_ref.at[pl.ds(first, block), :], fetched.at[pl.ds(pl.multiple_of(t * block, block), block), :], sem
        ).start()

    across = lax.broadcasted_iota(jnp.int32, (tokens, tokens), 1)
    along = lax.broadcasted_iota(jnp.int32, (tokens, tokens), 0)
    share = jnp.sum(
        jnp.where(routes_ref[...] == lax.axis_index("expert"), weights_ref[...], 0.0), axis=0, keepdims=True
    )
    share = jnp.sum(jnp.where(across == along, share, 0.0), axis=1, keepdims=True)
    local = jnp.sum(jnp.where(across == along, lane_ids_ref[...], 0), axis=1, keepdims=True) - base
    present = (local >= 0) & (local < shard_rows)
    place = lax.broadcasted_iota(jnp.int32, (tokens, 1), 0) * block + local % block
    place = jnp.where(present, place, -1)
    for k in range(groups):
        for d in range(experts):
            at = (d * groups + k) * dest_rows
            share_ref[k, d * dest_rows : (d + 1) * dest_rows, :] = share[at : at + dest_rows]
    pltpu.make_async_copy(fetched, fetched, sem).wait()
    spots = lax.broadcasted_iota(jnp.int32, (dest_rows, dest_rows * block), 1)
    for k in range(groups):
        for d in range(experts):
            at = (d * groups + k) * dest_rows
            pick = (spots + at * block == place[at : at + dest_rows]).astype(jnp.float32).astype(x_ref.dtype)
            value = jnp.dot(
                pick, fetched[at * block : (at + dest_rows) * block, :], preferred_element_type=jnp.float32
            ).astype(x_ref.dtype)
            for j in range(0, dest_rows, rows):
                x_ref[k, (d * dest_rows + j) // rows] = value[j : j + rows]


def gather(token_ids, routes, gate_weights, table, groups, size, rows):
    tokens, width = routes.shape[0], table.shape[1]
    block, experts = 8, lax.axis_size("expert")
    inside = pl.BlockSpec(memory_space=pltpu.VMEM)
    return pl.pallas_call(
        functools.partial(gather_kernel, (groups, size, rows, experts, block)),
        out_shape=(
            jax.ShapeDtypeStruct((groups, size, rows, width), table.dtype),
            jax.ShapeDtypeStruct((groups, size * rows, 1), jnp.float32),
        ),
        in_specs=[
            pl.BlockSpec(memory_space=pltpu.SMEM), inside, inside, inside, pl.BlockSpec(memory_space=pl.ANY)
        ],
        out_specs=(inside, inside),
        scratch_shapes=[pltpu.VMEM((tokens * block, width), table.dtype), pltpu.SemaphoreType.DMA],
        compiler_params=pltpu.CompilerParams(vmem_limit_bytes=VMEM_LIMIT - VMEM_ROOM),
    )(token_ids, token_ids.reshape(1, tokens), routes.T, gate_weights.T, table)


def token_groups(tokens, size, experts):
    for groups in (3, 2, 1):
        if tokens % (groups * size * 8) == 0 and tokens % (groups * experts * 8) == 0:
            return groups
    return 1


def per_device(token_ids, routes, gate_weights, embed_table, w_gate, w_up, w_down):
    vocab_rows, width = embed_table.shape
    tokens = routes.shape[0]
    experts = lax.axis_size("expert")
    size = lax.axis_size(GROUP)
    groups = token_groups(tokens, size, experts)
    rows = tokens // groups // size

    x, share = gather(token_ids, routes, gate_weights, embed_table, groups, size, rows)
    down = w_down[0]
    if width % 128:
        down = down.reshape(down.shape[0], experts, width).transpose(1, 0, 2)
    return fused(x, share, w_gate[0], w_up[0], down, embed_table, 0)


def solution(mesh):
    return jax.shard_map(
        per_device,
        mesh=mesh,
        in_specs=(
            P(),
            P(),
            P(),
            P(GROUP, "expert"),
            P("expert", None, GROUP),
            P("expert", None, GROUP),
            P("expert", GROUP, None),
        ),
        out_specs=P("expert", GROUP),
        check_vma=False,
    )
```

time: 138 us -> 110 us (0.80)
  local copies, waits for them, and re-layouts: 18.1 us -> 2.92 us
  Pallas kernels: 117 us -> 107 us
  other arithmetic: 3.07 us -> 0 us
    pallas_call x1, Pallas kernels: 117 us -> 102 us  [fused(): pl.pallas_call(functools.partial(fused_kernel, dims), out_shape=jax.Shape...]
    gather x1 -> x0, local copies, waits for them, and re-layouts: 14.9 us -> none  [per_device(): embed_table.at[jnp.clip(local_ids, 0, vocab_rows - 1)]]
    pallas_call x0 -> x1, Pallas kernels: none -> 5.37 us  [gather(): pl.pallas_call(functools.partial(gather_kernel, (groups, size, rows, expe...]
    unnamed x1 -> x7, local copies, waits for them, and re-layouts: 2.06 us -> 2.92 us
where the time goes in v2:
time: 110 us
  Pallas kernels  107 us (97%)
  local copies, waits for them, and re-layouts  2.92 us (3%)
    pallas_call x1, Pallas kernels, fused(): pl.pallas_call(functools.partial(fused_kernel, dims), out_shape=jax.Shape...  102 us
    pallas_call x1, Pallas kernels, gather(): pl.pallas_call(functools.partial(gather_kernel, (groups, size, rows, expe...  5.37 us
    unnamed x7, local copies, waits for them, and re-layouts  2.92 us

profile of v2, /device:TPU:0, one launch (start us, length us, event | category | flops | bytes accessed | tf_op | source)
XLA Modules:
  0.0 109.9 jit_solution(314443396183555945)
XLA Ops:
  0.0 0.0 copy-start
  0.0 0.7 copy-done
  0.7 0.0 copy-start.1
  0.7 0.7 copy-done.1
  1.4 0.0 copy-start.2
  1.4 0.7 copy-done.2
  2.0 5.4 %shard_map.73 = (bf16[3,8,8,1792]{3,2,1,0:T(8,128)(2,1)S(1)}, f32[3,64,1]{2,1,0:T(8,128)S(1)}) custom-call(s32[192]{0:T(256)S(1)} %copy-done, s32[1,192]{1,0:T(1,128)S(1)} %bitcast.6, s32[2,192]{1,0:T(2,128)S(1)} %bitcast.7, f32[2,192]{1,0:T(2,128)S(1)} %bitcast.8, bf16[8192,1792]{1,0:T(8,128)(2,1)} %table_ref.3), custom_call_target="tpu_custom_call" | custom-call | tf_op jit(solution)/shard_map/pallas_call | solution.py:492
  7.4 101.6 %shard_map.74 = bf16[48,8192]{1,0:T(8,128)(2,1)S(1)} custom-call(bf16[3,8,8,1792]{3,2,1,0:T(8,128)(2,1)S(1)} %get-tuple-element.7.x_ref, f32[3,64,1]{2,1,0:T(8,128)S(1)} %get-tuple-element.8.share_ref, bf16[7168,256]{1,0:T(8,128)(2,1)} %bitcast.9, bf16[7168,256]{1,0:T(8,128)(2,1)} %bitcast.10, bf16[256,7168]{1,0:T(8,128)(2,1)} %bitcast.11, ...), custom_call_target="tpu_custom_call" | custom-call | tf_op jit(solution)/shard_map/pallas_call | solution.py:415
  109.0 0.9 copy.9
Async XLA Ops:
  0.0 0.7 copy-start
  0.7 0.7 copy-start.1
  1.4 0.7 copy-start.2

commit v3 on v2

--- a/solution.py
+++ b/solution.py
@@ -16,8 +16,8 @@
 
 def fused_kernel(
     dims, x_ref, share_ref, gate_ref, up_ref, down_ref, table_ref, o_ref,
-    gate, up, down, tiles, scatter, mine, emb, paired, landed, summed, spread, res, held, right, left,
-    w_sem, t_sem, a_sem, b_sem, c_sem, n_sem, p_sem, d_sem, e_sem, f_sem, g_sem, x_sem, sent_rows, sent,
+    gate, up, down, tiles, couple, scatter, mine, emb, paired, landed, summed, spread, res, held, right, left,
+    w_sem, t_sem, h_sem, a_sem, b_sem, c_sem, n_sem, p_sem, d_sem, e_sem, f_sem, g_sem, x_sem, sent_rows, sent,
 ):
     pipes, vocabs, experts, groups, rows, width, tile, steps, buffers = dims
     chips = pipes * vocabs // 2
@@ -81,9 +81,16 @@
         return core * chips + (chip + c) % chips
 
     def start_scatter(k):
-        for i in range(1, size):
-            to = (me + i) % size
-            remote(x_ref.at[k, to], scatter.at[k, i - 1], sent.at[0], a_sem.at[k], at_rank(to)).start()
+        away = x_ref.at[k, pl.ds((1 - core) * chips, chips)]
+        remote(away, couple.at[k], sent.at[0], h_sem.at[k], partner).start()
+
+    def merge_scatter(k):
+        settle(couple.at[k], h_sem.at[k])
+        for c in range(chips):
+            couple[k, c] = (couple[k, c].astype(f32) + x_ref[k, core * chips + c].astype(f32)).astype(couple.dtype)
+        for c in range(1, chips):
+            block = couple.at[k, (chip + c) % chips]
+            remote(block, scatter.at[k, c - 1], sent.at[7], a_sem.at[k], at_rank(same_core(c))).start()
 
     def send_plane(k, i):
         b = (e + experts - i) % experts
@@ -93,9 +100,9 @@
         remote(src, emb.at[k, b, me], sent_rows.at[k], n_sem.at[k, i], partner).start()
 
     def own_rows(k):
-        total = x_ref[k, me].astype(f32)
+        total = couple[k, chip].astype(f32)
         settle(scatter.at[k], a_sem.at[k])
-        for i in range(size - 1):
+        for i in range(chips - 1):
             total = total + scatter[k, i].astype(f32)
         value = total.astype(mine.dtype)
         mine[k] = value
@@ -304,11 +311,13 @@
             phase(k)
 
     first = min(2, groups)
+    for k in range(groups):
+        run(start_scatter, k)
     for k in range(first):
-        run(start_scatter, k)
+        run(merge_scatter, k)
     run(own_rows, 0)
     for k in range(first, groups):
-        run(start_scatter, k)
+        run(merge_scatter, k)
     for k in range(1, first):
         run(own_rows, k)
     run(gather_rows, 0)
@@ -370,7 +379,8 @@
         def _(t):
             finish(last, t)
 
-    settle(scatter, sent.at[0])
+    settle(couple, sent.at[0])
+    settle(scatter, sent.at[7])
     settle(spread, sent.at[1])
     settle(paired, sent.at[2])
     settle(landed, sent.at[3])
@@ -399,7 +409,8 @@
         up.shape,
         (experts, hidden, width),
         (buffers, tile, width),
-        (groups, size - 1, rows, width),
+        (groups, chips, rows, width),
+        (groups, chips - 1, rows, width),
         (groups, rows, width),
         (groups, experts, size, rows, width),
         (groups, experts, chips, rows, width),
@@ -421,6 +432,7 @@
             dma((3,)),
             dma((buffers,)),
             dma((groups,)),
+            dma((groups,)),
             dma((groups, experts - 1)),
             dma((groups, experts)),
             dma((groups, experts)),
@@ -431,7 +443,7 @@
             dma((groups,)),
             dma((groups, experts + 1, steps)),
             dma((groups,)),
-            dma((7,)),
+            dma((8,)),
         ],
         compiler_params=pltpu.CompilerParams(
             collective_id=collective_id, has_side_effects=True,
@@ -440,7 +452,7 @@
     )(x, share, gate, up, down, table)
 
 
-def gather_kernel(dims, ids_ref, lane_ids_ref, routes_ref, weights_ref, table_ref, x_ref, share_ref, fetched, sem):
+def gather_kernel(dims, ids_ref, lane_ids_ref, lane_share_ref, table_ref, x_ref, share_ref, fetched, sem):
     groups, size, rows, experts, block = dims
     tokens = ids_ref.shape[0]
     width = table_ref.shape[1]
@@ -460,10 +472,7 @@
 
     across = lax.broadcasted_iota(jnp.int32, (tokens, tokens), 1)
     along = lax.broadcasted_iota(jnp.int32, (tokens, tokens), 0)
-    share = jnp.sum(
-        jnp.where(routes_ref[...] == lax.axis_index("expert"), weights_ref[...], 0.0), axis=0, keepdims=True
-    )
-    share = jnp.sum(jnp.where(across == along, share, 0.0), axis=1, keepdims=True)
+    share = jnp.sum(jnp.where(across == along, lane_share_ref[...], 0.0), axis=1, keepdims=True)
     local = jnp.sum(jnp.where(across == along, lane_ids_ref[...], 0), axis=1, keepdims=True) - base
     present = (local >= 0) & (local < shard_rows)
     place = lax.broadcasted_iota(jnp.int32, (tokens, 1), 0) * block + local % block
@@ -485,8 +494,8 @@
                 x_ref[k, (d * dest_rows + j) // rows] = value[j : j + rows]
 
 
-def gather(token_ids, routes, gate_weights, table, groups, size, rows):
-    tokens, width = routes.shape[0], table.shape[1]
+def gather(token_ids, share, table, groups, size, rows):
+    tokens, width = token_ids.shape[0], table.shape[1]
     block, experts = 8, lax.axis_size("expert")
     inside = pl.BlockSpec(memory_space=pltpu.VMEM)
     return pl.pallas_call(
@@ -496,12 +505,12 @@
             jax.ShapeDtypeStruct((groups, size * rows, 1), jnp.float32),
         ),
         in_specs=[
-            pl.BlockSpec(memory_space=pltpu.SMEM), inside, inside, inside, pl.BlockSpec(memory_space=pl.ANY)
+            pl.BlockSpec(memory_space=pltpu.SMEM), inside, inside, pl.BlockSpec(memory_space=pl.ANY)
         ],
         out_specs=(inside, inside),
         scratch_shapes=[pltpu.VMEM((tokens * block, width), table.dtype), pltpu.SemaphoreType.DMA],
         compiler_params=pltpu.CompilerParams(vmem_limit_bytes=VMEM_LIMIT - VMEM_ROOM),
-    )(token_ids, token_ids.reshape(1, tokens), routes.T, gate_weights.T, table)
+    )(token_ids, token_ids.reshape(1, tokens), share.reshape(1, tokens), table)
 
 
 def token_groups(tokens, size, experts):
@@ -519,7 +528,8 @@
     groups = token_groups(tokens, size, experts)
     rows = tokens // groups // size
 
-    x, share = gather(token_ids, routes, gate_weights, embed_table, groups, size, rows)
+    share = jnp.sum(jnp.where(routes == lax.axis_index("expert"), gate_weights, 0.0), axis=1)
+    x, share = gather(token_ids, share, embed_table, groups, size, rows)
     down = w_down[0]
     if width % 128:
         down = down.reshape(down.shape[0], experts, width).transpose(1, 0, 2)

time: 110 us -> 107 us (0.973)
  Pallas kernels: 107 us -> 105 us
  local copies, waits for them, and re-layouts: 2.92 us -> 1.56 us
    unnamed x7 -> x3, local copies, waits for them, and re-layouts: 2.92 us -> 1.56 us
    pallas_call x1, Pallas kernels: 5.37 us -> 4.24 us  [gather(): pl.pallas_call(functools.partial(gather_kernel, (groups, size, rows, expe...]
where the time goes in v3:
time: 107 us
  Pallas kernels  105 us (98%)
  local copies, waits for them, and re-layouts  1.56 us (1%)
    pallas_call x1, Pallas kernels, fused(): pl.pallas_call(functools.partial(fused_kernel, dims), out_shape=jax.Shape...  101 us
    pallas_call x1, Pallas kernels, gather(): pl.pallas_call(functools.partial(gather_kernel, (groups, size, rows, expe...  4.24 us

profile of v3, /device:TPU:0, one launch (start us, length us, event | category | flops | bytes accessed | tf_op | source)
XLA Modules:
  0.0 107.2 jit_solution(12997673815002203299)
XLA Ops:
  0.0 0.7 fusion
  0.7 0.0 copy-start
  0.7 0.7 copy-done
  1.4 4.2 %shard_map.73 = (bf16[3,8,8,1792]{3,2,1,0:T(8,128)(2,1)S(1)}, f32[3,64,1]{2,1,0:T(8,128)S(1)}) custom-call(s32[192]{0:T(256)S(1)} %copy-done, s32[1,192]{1,0:T(1,128)S(1)} %bitcast.5, f32[1,192]{1,0:T(1,128)S(1)} %bitcast.6, bf16[8192,1792]{1,0:T(8,128)(2,1)} %table_ref.3), custom_call_target="tpu_custom_call" | custom-call | tf_op jit(solution)/shard_map/pallas_call | solution.py:501
  5.6 100.6 %shard_map.74 = bf16[48,8192]{1,0:T(8,128)(2,1)S(1)} custom-call(bf16[3,8,8,1792]{3,2,1,0:T(8,128)(2,1)S(1)} %get-tuple-element.7.x_ref, f32[3,64,1]{2,1,0:T(8,128)S(1)} %get-tuple-element.8.share_ref, bf16[7168,256]{1,0:T(8,128)(2,1)} %bitcast.7, bf16[7168,256]{1,0:T(8,128)(2,1)} %bitcast.8, bf16[256,7168]{1,0:T(8,128)(2,1)} %bitcast.9, ...), custom_call_target="tpu_custom_call" | custom-call | tf_op jit(solution)/shard_map/pallas_call | solution.py:426
  106.3 0.9 copy.9
Async XLA Ops:
  0.7 0.7 copy-start
